TPU v7x, 512 devices: a whole 4x8x8 slice. The times are simulated.
512 devices in a mesh: rows: 128 (over y, z, core), rep: 4 (over x).
Axes of the slice: x: 4, y: 8, z: 8, core: 2. Of those that a mesh axis runs over, the one named last changes fastest.
Arguments:
- embed: bfloat16 [65536, 1024], P('rows'), may hold values from -6 to 6
- start: bfloat16 [65536, 128], P('rows'), may hold values from -6 to 6
- links: int32 [128, 128], P('rows'), may hold values from -1 to 3, as said below
Outputs:
- embedding: float32 [65536, 128], P('rows')
Inputs may be any that keep to these rules, and one draw needn't show every extreme that they name: `links`: entry [r, s] is -1 (no pair) or a block of owner s; the diagonal is -1; each row has at most 96 entries other than -1, and some row has exactly 96.
All inputs are finite; a program needn't handle non-finite values.
Results may differ from a plain program's by a relative error of at most 0.012.
Values may be sent and summed in bfloat16 or wider, within the bound.
No kernel may reach another device: no remote copies, remote signals or barrier semaphores. Data moves between devices by JAX's collectives and lax.ppermute only.
A program may use at most 128 MiB of HBM per device.

v0:
```python
import math

import jax
import jax.numpy as jnp
from jax import lax
from jax.sharding import PartitionSpec as P

BLOCK = 128
BLOCKS_DEV = 4
ITERS = 2


EPSILON = 1e-06


def from_everyone(shard, axis):
    copies = jnp.broadcast_to(shard, (lax.axis_size(axis), *shard.shape))
    return lax.all_to_all(copies, axis, split_axis=0, concat_axis=0, tiled=True)


def taken_together(shard, axis):
    everything = from_everyone(shard, axis)
    return jnp.sum(everything, axis=0)


def gathered_total(shard, axis):
    blocks = lax.all_gather(shard, axis)
    return blocks.sum(axis=0)


def row_scale(rows):
    values = rows.astype(jnp.float32)
    return lax.rsqrt(jnp.mean(values * values, axis=-1) + EPSILON)


def orthonormal(result, gram_matrix):
    lower_factor = jnp.linalg.cholesky(gram_matrix)
    return lax.linalg.triangular_solve(
        lower_factor, result, left_side=False, lower=True, transpose_a=True
    )


def quarter_of(values, blocks, rep_count, quarter_index):
    shaped = values.reshape(
        (blocks, rep_count, values.shape[0] // (blocks * rep_count)) + values.shape[1:]
    )
    return lax.dynamic_index_in_dim(shaped, quarter_index, 1, keepdims=False)


def widen(block_part, rep_count, quarter_index):
    choose = (jnp.arange(rep_count) == quarter_index).astype(jnp.float32)
    expanded = block_part[:, None] * choose.reshape((1, rep_count) + (1,) * (block_part.ndim - 1))
    return expanded.reshape((-1,) + block_part.shape[2:])


def on_device(embed, start, links):
    rows_count = lax.axis_size("rows")
    rep_count = lax.axis_size("rep")
    quarter_index = lax.axis_index("rep")
    slab_rows, feature_count = embed.shape
    comp_count = start.shape[1]
    blocks = BLOCKS_DEV
    piece_rows = BLOCK // rep_count
    link_max = max(1, 3 * rows_count // 4)
    spread = 2.0 / math.sqrt(feature_count)
    highest = lax.Precision.HIGHEST
    slab_scale = row_scale(embed)
    own_quarter = quarter_of(embed, blocks, rep_count, quarter_index)
    quarter_scale = row_scale(own_quarter)
    link_row = links.reshape(rows_count)
    alive_dense = (link_row >= 0).astype(jnp.float32)
    asked_for = lax.all_to_all(
        links.reshape(rows_count, 1), "rows", split_axis=0, concat_axis=0, tiled=True
    )[:, 0]
    picked = jnp.clip(asked_for, 0, blocks - 1)
    placer = (asked_for[:, None] == jnp.arange(blocks)[None, :]).astype(jnp.float32)
    outgoing = jnp.take(own_quarter, picked, axis=0)
    slot_order = jnp.argsort((link_row < 0).astype(jnp.int32), stable=True)[:link_max]
    slot_placer = (slot_order[:, None] == jnp.arange(rows_count)[None, :]).astype(jnp.float32)
    arrived = lax.all_to_all(outgoing, "rows", split_axis=0, concat_axis=0, tiled=True)
    pieces = jnp.take(arrived, slot_order, axis=0)
    piece_scale = row_scale(pieces)
    products_in = jnp.einsum("pnd,rd->pnr", pieces, embed, preferred_element_type=jnp.float32)
    exponent = spread * products_in * piece_scale[:, :, None] * slab_scale[None, None, :]
    pair_tiles = (jnp.exp(exponent) * alive_dense[slot_order][:, None, None]).astype(jnp.bfloat16)

    def to_owners(per_slot, form):
        return jnp.einsum(form, slot_placer, per_slot, precision=highest)

    diag_products = jnp.einsum(
        "bnd,rd->bnr", own_quarter, embed, preferred_element_type=jnp.float32
    )
    diag_exponent = spread * diag_products * quarter_scale[:, :, None] * slab_scale[None, None, :]
    row_ids = (
        jnp.arange(blocks)[:, None] * BLOCK
        + quarter_index * piece_rows
        + jnp.arange(piece_rows)[None, :]
    )
    self_mask = row_ids[:, :, None] == jnp.arange(slab_rows)[None, None, :]
    diag_tile = (
        jnp.where(self_mask, 0.0, jnp.exp(diag_exponent))
        .astype(jnp.bfloat16)
        .reshape(blocks * piece_rows, slab_rows)
    )
    own_sums = jnp.sum(pair_tiles, axis=(0, 1), dtype=jnp.float32) + jnp.sum(
        diag_tile, axis=0, dtype=jnp.float32
    )
    back_sums = to_owners(jnp.sum(pair_tiles, axis=2, dtype=jnp.float32), "mp,mn->pn")
    got_sums = lax.all_to_all(back_sums, "rows", split_axis=0, concat_axis=0, tiled=True)
    placed_sums = jnp.dot(placer.T, got_sums, precision=highest)
    degree = taken_together(own_sums + widen(placed_sums, rep_count, quarter_index), "rep")
    inv_root = lax.rsqrt(degree)
    current = start.astype(jnp.float32)
    scaled = (current * inv_root[:, None]).astype(jnp.bfloat16)
    for turn_index in range(ITERS):
        scaled_quarter = quarter_of(scaled, blocks, rep_count, quarter_index)
        outgoing_iterate = jnp.take(scaled_quarter, picked, axis=0)
        reverse = jnp.einsum("pnr,rk->pnk", pair_tiles, scaled, preferred_element_type=jnp.float32)
        returned = lax.all_to_all(
            to_owners(reverse, "mp,mnk->pnk"), "rows", split_axis=0, concat_axis=0, tiled=True
        )
        fetched = jnp.take(
            lax.all_to_all(outgoing_iterate, "rows", split_axis=0, concat_axis=0, tiled=True),
            slot_order,
            axis=0,
        )
        forward = lax.dot_general(
            pair_tiles, fetched, (((0, 1), (0, 1)), ((), ())), preferred_element_type=jnp.float32
        )
        forward = forward + lax.dot_general(
            diag_tile,
            scaled_quarter.reshape(blocks * piece_rows, comp_count),
            (((0,), (0,)), ((), ())),
            preferred_element_type=jnp.float32,
        )
        placed = jnp.einsum("pb,pnk->bnk", placer, returned, precision=highest)
        summed_part = forward + widen(placed, rep_count, quarter_index)
        summed_all = taken_together(summed_part, "rep")
        result = summed_all * inv_root[:, None]
        gram_matrix = gathered_total(jnp.dot(result.T, result, precision=highest), "rows")
        current = orthonormal(result, gram_matrix)
        scaled = (current * inv_root[:, None]).astype(jnp.bfloat16)
    return current * math.sqrt(slab_rows * rows_count)


def solution(mesh):
    return jax.shard_map(
        on_device,
        mesh=mesh,
        in_specs=(P("rows", None), P("rows", None), P("rows", None)),
        out_specs=P("rows", None),
        check_vma=False,
    )
```

profile of v0, /device:TPU:1, one launch (start us, length us, event | category | flops | bytes accessed | tf_op | source)
XLA Modules:
  0.0 839.7 jit_solution(1342863353658587619)
XLA Ops:
  6.5 1.4 copy.85
  7.9 18.4 %all-to-all-start = ((s32[128,1,1]{2,1,0:T(1,128)}), s32[128,1,1]{2,1,0:T(1,128)S(1)}, u32[]{:S(2)}, u32[]{:S(2)}) async-start(s32[128,1,1]{2,1,0:T(1,128)} %copy.85), calls=%async_computation | async-start | bytes 131072 | tf_op jit(solution)/shard_map/all_to_all | solution.py:72
  26.3 1.1 multiply_reduce_fusion.2
  27.4 10.4 %all-to-all-done = s32[128,1,1]{2,1,0:T(1,128)S(1)} async-done(((s32[128,1,1]{2,1,0:T(1,128)}), s32[128,1,1]{2,1,0:T(1,128)S(1)}, u32[]{:S(2)}, u32[]{:S(2)}) %all-to-all-start) | async-done | bytes 544 | tf_op jit(solution)/shard_map/all_to_all | solution.py:72
  37.8 4.6 fusion.67
  42.5 6.4 gather_fusion
  49.0 7.4 broadcast_select_fusion
  56.4 7.5 all-to-all-start.1
  63.9 2.5 sort.17
  66.4 1.2 gather_fusion.2
  68.0 0.5 convert_reduce_fusion.2
  68.6 215.9 %all-to-all-done.1 = bf16[128,32,1024]{2,1,0:T(8,128)(2,1)} async-done(((bf16[128,32,1024]{2,1,0:T(8,128)(2,1)}), bf16[128,32,1024]{2,1,0:T(8,128)(2,1)}, u32[]{:S(2)}, u32[]{:S(2)}) %all-to-all-start.1) | async-done | bytes 8388640 | tf_op jit(solution)/shard_map/all_to_all | solution.py:80
  284.5 9.4 %gather_fusion.1 = bf16[96,32,1024]{2,1,0:T(8,128)(2,1)} fusion(bf16[128,32,1024]{2,1,0:T(8,128)(2,1)} %all-to-all-done.1, s32[1024]{0:T(1024)S(1)} %pad_clamp_fusion.1), kind=kCustom, calls=%fused_computation.5 | custom fusion | bytes 12583296 | tf_op jit(solution)/shard_map/jit(_take)/gather | solution.py:81
  294.0 4.7 multiply_reduce_fusion
  298.7 5.9 convert_reduce_fusion.1
  304.6 0.9 fusion.46
  305.5 43.2 %all-to-all-start.2 = ((f32[128,1,32]{2,1,0:T(1,128)}), f32[128,1,32]{2,1,0:T(1,128)S(1)}, u32[]{:S(2)}, u32[]{:S(2)}) async-start(f32[128,1,32]{2,1,0:T(1,128)} %bitcast.37), calls=%async_computation.2 | async-start | bytes 131072 | tf_op jit(solution)/shard_map/all_to_all | solution.py:109
  349.0 11.2 %all-to-all-done.2 = f32[128,1,32]{2,1,0:T(1,128)S(1)} async-done(((f32[128,1,32]{2,1,0:T(1,128)}), f32[128,1,32]{2,1,0:T(1,128)S(1)}, u32[]{:S(2)}, u32[]{:S(2)}) %all-to-all-start.2) | async-done | bytes 16416 | tf_op jit(solution)/shard_map/all_to_all | solution.py:109
  360.4 0.6 broadcast_in_dim.80
  361.1 4.0 all-to-all-start.3
  365.1 4.2 all-to-all-done.3
  369.4 0.8 gather_fusion.3
  370.2 1.2 broadcast_select_fusion.3
  371.4 7.7 all-to-all-start.4
  379.0 5.4 fusion.2
  384.5 1.1 fusion.49
  385.6 2.6 copy.93
  388.2 21.3 %all-to-all-done.4 = bf16[128,32,128]{2,1,0:T(8,128)(2,1)S(1)} async-done(((bf16[128,32,128]{2,1,0:T(8,128)(2,1)}), bf16[128,32,128]{2,1,0:T(8,128)(2,1)S(1)}, u32[]{:S(2)}, u32[]{:S(2)}) %all-to-all-start.4) | async-done | bytes 1048608 | tf_op jit(solution)/shard_map/all_to_all | solution.py:123
  409.4 7.0 all-to-all-start.5
  416.5 1.6 gather_fusion.4
  418.1 3.3 convolution_bitcast_fusion.3
  421.5 47.3 %all-to-all-done.5 = f32[128,32,128]{2,1,0:T(8,128)S(1)} async-done(((f32[128,32,128]{2,1,0:T(8,128)}), f32[128,32,128]{2,1,0:T(8,128)S(1)}, u32[]{:S(2)}, u32[]{:S(2)}) %all-to-all-start.5) | async-done | bytes 2097184 | tf_op jit(solution)/shard_map/all_to_all | solution.py:119
  468.7 2.0 fusion.6
  471.1 16.7 %all_to_all.65 = f32[4,512,128]{2,1,0:T(8,128)S(1)} all-to-all(f32[4,512,128]{2,1,0:T(8,128)S(1)} %broadcast_in_dim.81), channel_id=1, replica_groups=mesh['rows'=128,'rep'=4] {'rep'}, dimensions={0} | all-to-all | bytes 2097152 | tf_op jit(solution)/shard_map/all_to_all | solution.py:18
  488.1 1.0 fusion.29
  489.1 82.6 %all-gather.5.cloned.1.call-done = f32[16384,128]{1,0:T(8,128)} async-done(((f32[128,128]{1,0:T(8,128)}), f32[16384,128]{1,0:T(8,128)}) %all-gather.5.cloned.1.call-update) | async-done | bytes 8388624 | tf_op jit(solution)/shard_map/all_gather | solution.py:27
  571.7 3.8 reduce_sum.107
  575.6 11.7 %cholesky.44 = f32[128,128]{1,0:T(8,128)S(1)} custom-call(f32[128,128]{1,0:T(8,128)S(1)} %fusion.42), custom_call_target="Cholesky" | custom-call | tf_op jit(solution)/shard_map/jit(cholesky)/cholesky | solution.py:37
  587.4 0.6 compare_reduce_fusion.1
  588.0 0.7 fusion.37
  588.7 9.8 %custom-call.6 = f32[1,128,128]{1,2,0:T(8,128)S(1)} custom-call(f32[1,128,128]{2,1,0:T(8,128)S(1)} %fusion.37), custom_call_target="InvertDiagBlocksLowerTriangular" | custom-call | tf_op jit(solution)/shard_map/triangular_solve/custom-call.0 | solution.py:38
  598.5 0.4 fusion.15
  599.0 0.8 gather_fusion.5
  599.8 1.2 broadcast_select_fusion.4
  601.0 9.3 %all-to-all-start.7 = ((bf16[128,32,128]{2,1,0:T(8,128)(2,1)}), bf16[128,32,128]{2,1,0:T(8,128)(2,1)S(1)}, u32[]{:S(2)}, u32[]{:S(2)}) async-start(bf16[128,32,128]{2,1,0:T(8,128)(2,1)} %broadcast_select_fusion.4), calls=%async_computation.7 | async-start | bytes 2097152 | tf_op jit(solution)/shard_map/all_to_all | solution.py:123
  610.3 5.4 fusion
  615.7 1.1 fusion.47
  616.9 2.6 copy.101
  619.5 21.2 %all-to-all-done.7 = bf16[128,32,128]{2,1,0:T(8,128)(2,1)S(1)} async-done(((bf16[128,32,128]{2,1,0:T(8,128)(2,1)}), bf16[128,32,128]{2,1,0:T(8,128)(2,1)S(1)}, u32[]{:S(2)}, u32[]{:S(2)}) %all-to-all-start.7) | async-done | bytes 1048608 | tf_op jit(solution)/shard_map/all_to_all | solution.py:123
  640.7 7.0 all-to-all-start.8
  647.8 1.6 gather_fusion.6
  649.4 3.3 convolution_bitcast_fusion.2
  652.7 47.2 %all-to-all-done.8 = f32[128,32,128]{2,1,0:T(8,128)S(1)} async-done(((f32[128,32,128]{2,1,0:T(8,128)}), f32[128,32,128]{2,1,0:T(8,128)S(1)}, u32[]{:S(2)}, u32[]{:S(2)}) %all-to-all-start.8) | async-done | bytes 2097184 | tf_op jit(solution)/shard_map/all_to_all | solution.py:119
  699.9 2.0 fusion.4
  702.4 17.6 %all_to_all.66 = f32[4,512,128]{2,1,0:T(8,128)S(1)} all-to-all(f32[4,512,128]{2,1,0:T(8,128)S(1)} %broadcast_in_dim.82), channel_id=1, replica_groups=mesh['rows'=128,'rep'=4] {'rep'}, dimensions={0} | all-to-all | bytes 2097152 | tf_op jit(solution)/shard_map/all_to_all | solution.py:18
  720.1 1.0 fusion.26
  721.2 83.2 %all-gather.7.cloned.1.call-done = f32[16384,128]{1,0:T(8,128)} async-done(((f32[128,128]{1,0:T(8,128)}), f32[16384,128]{1,0:T(8,128)}) %all-gather.7.cloned.1.call-update) | async-done | bytes 8388624 | tf_op jit(solution)/shard_map/all_gather | solution.py:27
  804.3 3.8 reduce_sum.109
  808.3 11.7 %cholesky.55 = f32[128,128]{1,0:T(8,128)S(1)} custom-call(f32[128,128]{1,0:T(8,128)S(1)} %fusion.40), custom_call_target="Cholesky" | custom-call | tf_op jit(solution)/shard_map/jit(cholesky)/cholesky | solution.py:37
  820.0 0.6 compare_reduce_fusion
  820.6 0.7 fusion.38
  821.3 9.8 %custom-call.7 = f32[1,128,128]{1,2,0:T(8,128)S(1)} custom-call(f32[1,128,128]{2,1,0:T(8,128)S(1)} %fusion.38), custom_call_target="InvertDiagBlocksLowerTriangular" | custom-call | tf_op jit(solution)/shard_map/triangular_solve/custom-call.0 | solution.py:38
  831.1 0.4 fusion.10
  831.6 0.8 copy.106
  (61 shorter events, 2.9 us)
Async XLA Ops:
  7.9 29.9 %all-to-all-start = ((s32[128,1,1]{2,1,0:T(1,128)}), s32[128,1,1]{2,1,0:T(1,128)S(1)}, u32[]{:S(2)}, u32[]{:S(2)}) async-start(s32[128,1,1]{2,1,0:T(1,128)} %copy.85), calls=%async_computation | async-start | bytes 131072 | tf_op jit(solution)/shard_map/all_to_all | solution.py:72
  56.4 7.5 copy-start.3
  56.4 11.3 %copy-start.1 = (bf16[512,1024]{1,0:T(8,128)(2,1)S(1)}, bf16[512,1024]{1,0:T(8,128)(2,1)}, u32[]{:S(2)}) copy-start(bf16[512,1024]{1,0:T(8,128)(2,1)} %param.10) | copy-start | bytes 3145732
  56.4 228.2 %all-to-all-start.1 = ((bf16[128,32,1024]{2,1,0:T(8,128)(2,1)}), bf16[128,32,1024]{2,1,0:T(8,128)(2,1)}, u32[]{:S(2)}, u32[]{:S(2)}) async-start(bf16[128,32,1024]{2,1,0:T(8,128)(2,1)} %broadcast_select_fusion), calls=%async_computation.1 | async-start | bytes 16777216 | tf_op jit(solution)/shard_map/all_to_all | solution.py:80
  294.0 4.7 copy-start
  298.7 50.1 %copy-start.2 = (bf16[512,128]{1,0:T(8,128)(2,1)S(1)}, bf16[512,128]{1,0:T(8,128)(2,1)}, u32[]{:S(2)}) copy-start(bf16[512,128]{1,0:T(8,128)(2,1)} %param.11) | copy-start | bytes 393220
  305.5 54.7 %all-to-all-start.2 = ((f32[128,1,32]{2,1,0:T(1,128)}), f32[128,1,32]{2,1,0:T(1,128)S(1)}, u32[]{:S(2)}, u32[]{:S(2)}) async-start(f32[128,1,32]{2,1,0:T(1,128)} %bitcast.37), calls=%async_computation.2 | async-start | bytes 131072 | tf_op jit(solution)/shard_map/all_to_all | solution.py:109
  361.1 8.2 all-to-all-start.3
  371.4 38.1 %all-to-all-start.4 = ((bf16[128,32,128]{2,1,0:T(8,128)(2,1)}), bf16[128,32,128]{2,1,0:T(8,128)(2,1)S(1)}, u32[]{:S(2)}, u32[]{:S(2)}) async-start(bf16[128,32,128]{2,1,0:T(8,128)(2,1)} %broadcast_select_fusion.3), calls=%async_computation.4 | async-start | bytes 2097152 | tf_op jit(solution)/shard_map/all_to_all | solution.py:123
  409.4 59.3 %all-to-all-start.5 = ((f32[128,32,128]{2,1,0:T(8,128)}), f32[128,32,128]{2,1,0:T(8,128)S(1)}, u32[]{:S(2)}, u32[]{:S(2)}) async-start(f32[128,32,128]{2,1,0:T(8,128)} %copy.93), calls=%async_computation.5 | async-start | bytes 4194304 | tf_op jit(solution)/shard_map/all_to_all | solution.py:119
  416.5 155.2 %all-gather.5.cloned.1.call-start = ((), (), s32[]{:S(2)}) async-start(), calls=%async_computation.10 | async-start | bytes 8454144 | tf_op jit(solution)/shard_map/all_gather | solution.py:27
  601.0 39.7 %all-to-all-start.7 = ((bf16[128,32,128]{2,1,0:T(8,128)(2,1)}), bf16[128,32,128]{2,1,0:T(8,128)(2,1)S(1)}, u32[]{:S(2)}, u32[]{:S(2)}) async-start(bf16[128,32,128]{2,1,0:T(8,128)(2,1)} %broadcast_select_fusion.4), calls=%async_computation.7 | async-start | bytes 2097152 | tf_op jit(solution)/shard_map/all_to_all | solution.py:123
  640.7 59.3 %all-to-all-start.8 = ((f32[128,32,128]{2,1,0:T(8,128)}), f32[128,32,128]{2,1,0:T(8,128)S(1)}, u32[]{:S(2)}, u32[]{:S(2)}) async-start(f32[128,32,128]{2,1,0:T(8,128)} %copy.101), calls=%async_computation.8 | async-start | bytes 4194304 | tf_op jit(solution)/shard_map/all_to_all | solution.py:119
  647.7 156.6 %all-gather.7.cloned.1.call-start = ((), (), s32[]{:S(2)}) async-start(), calls=%async_computation.11 | async-start | bytes 8454144 | tf_op jit(solution)/shard_map/all_gather | solution.py:27
Sparse Core Ops, SparseCore 0:
  489.2 82.4 all-gather.4
  721.3 82.9 all-gather.6
where the time goes:
time: 848 us; the launch traced here: 840 us
  waiting for transfers between devices  544 us (64%)
  starting transfers between devices  104 us (12%)
  other arithmetic  77 us (9%)
  matrix products  34.5 us (4%)
  blocking collectives  34.3 us (4%)
  local copies, waits for them, and re-layouts  31.1 us (4%)
  between operations  14.3 us (2%)
    all_to_all x1, waiting for transfers between devices, on_device(): lax.all_to_all(outgoing, 'rows', split_axis=0, concat_axis=0, tiled=True)  216 us
    all_gather x2, waiting for transfers between devices, gathered_total(): blocks = lax.all_gather(shard, axis)  166 us
    all_to_all x2, waiting for transfers between devices, on_device(): lax.all_to_all(to_owners(reverse, 'mp,mnk->pnk'), 'rows', split_axis=0, c...  94.5 us
    all_to_all x1, starting transfers between devices, on_device(): lax.all_to_all(back_sums, 'rows', split_axis=0, concat_axis=0, tiled=True)  43.2 us
    all_to_all x2, waiting for transfers between devices, on_device(): lax.all_to_all(outgoing_iterate, 'rows', split_axis=0, concat_axis=0, til...  42.5 us
    all_to_all x2, blocking collectives, from_everyone(): return lax.all_to_all(copies, axis, split_axis=0, concat_axis=0, tiled=True)  34.3 us
    another operation x6, other arithmetic, orthonormal(): lower_factor = jnp.linalg.cholesky(gram_matrix)  24.8 us
    another operation x4, other arithmetic, orthonormal(): lax.linalg.triangular_solve(lower_factor, result, left_side=False, lower=...  20.9 us
  transfers between devices with their start and end apart: 10, of which 10 were waited for; matrix products, arithmetic and copies ran while one was open for 4% of the time, Pallas kernels for 0%

commit v1 on v0

v1 whole, which is shorter than its diff:
```python
import math

import jax
import jax.numpy as jnp
from jax import lax
from jax.sharding import Mesh, PartitionSpec as P

BLOCK = 128
BLOCKS_DEV = 4
ITERS = 2
EPSILON = 1e-06
ROWS = ("y", "z", "c")


def row_scale(rows):
    values = rows.astype(jnp.float32)
    return lax.rsqrt(jnp.mean(values * values, axis=-1) + EPSILON)


def orthonormal(result, gram_matrix):
    lower_factor = jnp.linalg.cholesky(gram_matrix)
    return lax.linalg.triangular_solve(
        lower_factor, result, left_side=False, lower=True, transpose_a=True
    )


def pair_counts(table, y_count, z_count):
    y, z, c, x = (lax.axis_index(name) for name in ("y", "z", "c", "x"))
    by_place = table.reshape(y_count, z_count, 2, y_count, z_count, 2)
    ahead = by_place[y, :, c][:, :, z]
    back = by_place[:, z, :, y, :, c]
    back = jnp.transpose(back, (2, 0, 1))
    blocks = jnp.arange(BLOCKS_DEV)
    same = (
        (jnp.arange(z_count)[:, None, None] == z)
        & (jnp.arange(y_count)[None, :, None] == y)
        & (jnp.arange(2)[None, None, :] == c)
    )
    counts = (
        (ahead == x).astype(jnp.float32)[:, None]
        + (back[:, None] == blocks[None, :, None, None]).astype(jnp.float32)
        + same.astype(jnp.float32)[:, None]
    )
    return counts.reshape(z_count * BLOCKS_DEV, y_count * 2)


def on_device(embed, start, links):
    y_count, z_count = lax.axis_size("y"), lax.axis_size("z")
    y, z, c, x = (lax.axis_index(name) for name in ("y", "z", "c", "x"))
    slab_rows, feature_count = embed.shape
    points = slab_rows * y_count * z_count * 2
    spread = 2.0 / math.sqrt(feature_count)
    highest = lax.Precision.HIGHEST

    own = lax.dynamic_slice_in_dim(embed, x * BLOCK, BLOCK, 0)
    table = lax.all_gather(links, ROWS, axis=0, tiled=True)
    cols = lax.all_gather(own, ("y", "c"), axis=0, tiled=True)
    rows = lax.all_gather(own, ("z", "x"), axis=0, tiled=True)
    counts = pair_counts(table, y_count, z_count)
    products = lax.dot_general(
        rows, cols, (((1,), (1,)), ((), ())), preferred_element_type=jnp.float32
    )
    exponent = spread * products * row_scale(rows)[:, None] * row_scale(cols)[None, :]
    row_ids = jnp.arange(rows.shape[0])[:, None]
    col_ids = jnp.arange(cols.shape[0])[None, :]
    offset = (z * BLOCKS_DEV + x) * BLOCK - (y * 2 + c) * BLOCK
    on_diagonal = (row_ids - col_ids == offset) & (col_ids // BLOCK == y * 2 + c)
    weight = jnp.repeat(jnp.repeat(counts, BLOCK, axis=0), BLOCK, axis=1)
    weight = jnp.where(on_diagonal, 0.0, weight)
    tile = (jnp.exp(exponent) * weight).astype(jnp.bfloat16)
    sums = jnp.sum(tile, axis=1, dtype=jnp.float32).reshape(-1, BLOCK)
    got = lax.all_to_all(sums, ("z", "x"), split_axis=0, concat_axis=0, tiled=True)
    inv_root = lax.rsqrt(jnp.sum(got, axis=0))[:, None]

    current = lax.dynamic_slice_in_dim(start, x * BLOCK, BLOCK, 0).astype(jnp.float32)
    for turn in range(ITERS):
        scaled = (current * inv_root).astype(jnp.bfloat16)
        fetched = lax.all_gather(scaled, ("y", "c"), axis=0, tiled=True)
        part = jnp.dot(tile, fetched, preferred_element_type=jnp.float32)
        total = lax.psum_scatter(part, ("z", "x"), scatter_dimension=0, tiled=True)
        result = total * inv_root
        gram = lax.psum(jnp.dot(result.T, result, precision=highest), ("y", "z", "c", "x"))
        if turn == ITERS - 1:
            result = lax.all_gather(result, "x", axis=0, tiled=True)
        current = orthonormal(result, gram)
    return current * math.sqrt(points)


def solution(mesh):
    owners, reps = mesh.devices.shape
    side = math.isqrt(owners // 2)
    fine = Mesh(mesh.devices.reshape(side, side, 2, reps), ("y", "z", "c", "x"))
    return jax.shard_map(
        on_device,
        mesh=fine,
        in_specs=(P(ROWS, None), P(ROWS, None), P(ROWS, None)),
        out_specs=P(ROWS, None),
        check_vma=False,
    )
```

time: 848 us -> 1300 us (1.53)
  waiting for transfers between devices: 544 us -> 1040 us
  starting transfers between devices: 104 us -> 0.21 us
  blocking collectives: 34.3 us -> 113 us
  matrix products: 34.5 us -> 59.1 us
  other arithmetic: 77 us -> 58.4 us
  local copies, waits for them, and re-layouts: 31.1 us -> 13 us
    psum x0 -> x2, waiting for transfers between devices: none -> 530 us  [on_device(): lax.psum(jnp.dot(result.T, result, precision=highest), ('y', 'z', 'c', 'x'))]
    reduce_scatter x0 -> x2, waiting for transfers between devices: none -> 422 us  [on_device(): total = lax.psum_scatter(part, ('z', 'x'), scatter_dimension=0, tiled=True)]
    all_to_all x8 -> x0, waiting for transfers between devices: 379 us -> none  [the longest x1 216 us: on_device(): lax.all_to_all(outgoing, 'rows', split_axis=0, concat_axis=0, tiled=True)]
    all_to_all x8 -> x0, starting transfers between devices: 104 us -> none  [the longest x1 43.2 us: on_device(): lax.all_to_all(back_sums, 'rows', split_axis=0, concat_axis=0, tiled=True)]
    all_gather x0 -> x4, blocking collectives: none -> 99.6 us  [the longest x1 52.2 us: on_device(): table = lax.all_gather(links, ROWS, axis=0, tiled=True)]
    all_gather x2, waiting for transfers between devices: 166 us -> 89.8 us  [the longest x1 89.7 us: on_device(): rows = lax.all_gather(own, ('z', 'x'), axis=0, tiled=True)]
    dot_general x14 -> x3, matrix products: 31.6 us -> 54.1 us  [the longest x1 35.1 us: on_device(): lax.dot_general(rows, cols, (((1,), (1,)), ((), ())), preferred_element_t...]
    gather x7 -> x0, local copies, waits for them, and re-layouts: 21.8 us -> none  [the longest x1 9.44 us: on_device(): pieces = jnp.take(arrived, slot_order, axis=0)]
  transfers between devices with their start and end apart: 10 -> 6, of which waited for: 10 -> 5; matrix products, arithmetic and copies ran while one was open for 4% -> 1% of each run, Pallas kernels for 0% -> 0%
where the time goes in v1:
time: 1300 us
  waiting for transfers between devices  1040 us (80%)
  blocking collectives  113 us (9%)
  matrix products  59.1 us (5%)
  other arithmetic  58.4 us (4%)
  between operations  13.7 us (1%)
  local copies, waits for them, and re-layouts  13 us (1%)
    psum x2, waiting for transfers between devices, on_device(): lax.psum(jnp.dot(result.T, result, precision=highest), ('y', 'z', 'c', 'x'))  530 us
    reduce_scatter x2, waiting for transfers between devices, on_device(): total = lax.psum_scatter(part, ('z', 'x'), scatter_dimension=0, tiled=True)  422 us
    all_gather x1, waiting for transfers between devices, on_device(): rows = lax.all_gather(own, ('z', 'x'), axis=0, tiled=True)  89.7 us
    all_gather x1, blocking collectives, on_device(): table = lax.all_gather(links, ROWS, axis=0, tiled=True)  52.2 us
    all_gather x2, blocking collectives, on_device(): fetched = lax.all_gather(scaled, ('y', 'c'), axis=0, tiled=True)  38.1 us
    dot_general x1, matrix products, on_device(): lax.dot_general(rows, cols, (((1,), (1,)), ((), ())), preferred_element_t...  35.1 us
  transfers between devices with their start and end apart: 6, of which 5 were waited for; matrix products, arithmetic and copies ran while one was open for 1% of the time, Pallas kernels for 0%

profile of v1, /device:TPU:1, one launch (start us, length us, event | category | flops | bytes accessed | tf_op | source)
XLA Modules:
  0.0 1300.7 jit_solution(8653269757164486245)
XLA Ops:
  6.5 1.2 copy-done
  7.8 0.7 constant_dynamic-slice_fusion.2
  8.5 0.0 all-gather.4.cloned.1.call-start
  8.6 0.7 all-gather.4.cloned.1.call-update
  9.3 0.0 reduce-scatter.3.cloned.1.call-start
  9.3 0.1 eq.90
  9.4 0.1 broadcast_and_fusion
  9.5 0.1 and_convert_fusion
  9.6 0.1 add.109
  9.7 0.1 add.110
  9.8 52.2 %all-gather = s32[128,1,128]{2,1,0:T(1,128)S(1)} all-gather(s32[1,1,128]{2,1,0:T(1,128)} %bitcast.64), channel_id=1, replica_groups=mesh['y'=8,'z'=8,'c'=2,'x'=4] {'y','z','c'}, dimensions={0}, use_global_device_ids=true | all-gather | bytes 66048 | tf_op jit(solution)/shard_map/all_gather | solution.py:56
  61.9 0.6 broadcast.169
  62.5 0.8 reduce.8
  63.4 5.5 reshape.143
  68.9 0.9 constant_dynamic-slice_fusion
  69.8 0.2 copy.47
  70.0 1.0 constant_dynamic-slice_fusion.1
  71.0 0.1 copy.56
  71.1 0.1 copy.46
  71.2 0.1 eq.87
  71.3 0.1 eq.88
  71.4 0.1 add.106
  71.4 0.1 add.107
  71.5 0.1 broadcast_in_dim.8
  71.7 0.2 copy.59
  71.9 0.0 all-gather.6.cloned.1.call-done
  71.9 3.1 multiply_reduce_fusion.1
  75.0 89.7 %all-gather.4.cloned.1.call-done = bf16[4096,1024]{1,0:T(8,128)(2,1)} async-done(((bf16[128,1024]{1,0:T(8,128)(2,1)}), bf16[4096,1024]{1,0:T(8,128)(2,1)}) %all-gather.4.cloned.1.call-update) | async-done | bytes 8388624 | tf_op jit(solution)/shard_map/all_gather | solution.py:58
  164.7 5.1 multiply_reduce_fusion
  169.8 35.1 %convert_reduce_fusion = (f32[4096]{0:T(1024)S(1)}, bf16[4096,2048]{0,1:T(8,128)(2,1)}) fusion(f32[4096,16]{0,1:T(8,128)S(1)} %bitcast.60, pred[2048]{0:T(1024)(128)(4,1)S(1)} %fusion.15, s32[]{:T(128)S(6)} %sub.25, f32[2048]{0:T(1024)S(1)} %add_rsqrt_fusion, f32[4096]{0:T(1024)S(1)} %rsqrt_multiply_fusion, ...), kind=kOutput, calls=%fused_computation.3 | convolution fusion | flops 17263751168 | bytes 29665284 | tf_op jit(solution)/shard_map/dot_general | solution.py:60
  204.9 13.6 %all_to_all.9 = f32[32,1,128]{2,1,0:T(1,128)S(1)} all-to-all(f32[32,1,128]{2,1,0:T(1,128)S(1)} %bitcast.63), channel_id=1, replica_groups=mesh['y'=8,'z'=8,'c'=2,'x'=4] {'z','x'}, dimensions={0} | all-to-all | bytes 32768 | tf_op jit(solution)/shard_map/all_to_all | solution.py:72
  218.5 0.8 multiply_convert_fusion
  219.3 21.1 %all_gather.21 = bf16[2048,128]{1,0:T(8,128)(2,1)S(1)} all-gather(bf16[128,128]{1,0:T(8,128)(2,1)S(1)} %multiply_convert_fusion), channel_id=1, replica_groups=mesh['y'=8,'z'=8,'c'=2,'x'=4] {'y','c'}, dimensions={0}, use_global_device_ids=true | all-gather | bytes 557056 | tf_op jit(solution)/shard_map/all_gather | solution.py:78
  240.4 9.5 fusion.19
  249.9 0.0 reduce-scatter.3.cloned.1.call-update
  249.9 0.0 all-reduce.3.cloned.1.call-start
  250.0 210.9 %reduce-scatter.3.cloned.1.call-done = f32[128,128]{1,0:T(8,128)} async-done(((f32[4096,128]{1,0:T(8,128)}), f32[128,128]{1,0:T(8,128)}) %reduce-scatter.3.cloned.1.call-update) | async-done | bytes 65552 | tf_op jit(solution)/shard_map/reduce_scatter | solution.py:80
  460.8 1.9 fusion.11
  462.7 0.0 all-reduce.3.cloned.1.call-update
  462.8 0.0 reduce-scatter.5.cloned.1.call-start
  462.8 269.7 %all-reduce.3.cloned.1.call-done = f32[128,128]{0,1:T(8,128)} async-done(((f32[128,128]{0,1:T(8,128)}), f32[128,128]{0,1:T(8,128)}) %all-reduce.3.cloned.1.call-update) | async-done | bytes 65552 | tf_op jit(solution)/shard_map/psum | solution.py:82
  732.5 0.9 copy.51
  733.4 0.9 fusion.9
  734.3 11.7 cholesky.44
  746.0 0.6 compare_reduce_fusion.1
  746.7 0.7 fusion.4
  747.3 9.8 custom-call.8
  757.2 1.1 fusion.3
  758.3 17.0 %all_gather.22 = bf16[2048,128]{1,0:T(8,128)(2,1)S(1)} all-gather(bf16[128,128]{1,0:T(8,128)(2,1)S(1)} %fusion.3), channel_id=1, replica_groups=mesh['y'=8,'z'=8,'c'=2,'x'=4] {'y','c'}, dimensions={0}, use_global_device_ids=true | all-gather | bytes 557056 | tf_op jit(solution)/shard_map/all_gather | solution.py:78
  775.3 9.5 fusion.20
  784.8 0.0 reduce-scatter.5.cloned.1.call-update
  784.8 0.0 all-reduce.5.cloned.1.call-start
  784.9 211.6 %reduce-scatter.5.cloned.1.call-done = f32[128,128]{1,0:T(8,128)} async-done(((f32[4096,128]{1,0:T(8,128)}), f32[128,128]{1,0:T(8,128)}) %reduce-scatter.5.cloned.1.call-update) | async-done | bytes 65552 | tf_op jit(solution)/shard_map/reduce_scatter | solution.py:80
  996.5 0.9 broadcast_multiply_fusion
  997.4 0.9 fusion.21
  998.3 9.4 all_gather.23
  1007.7 260.4 %all-reduce.5.cloned.1.call-done = f32[128,128]{0,1:T(8,128)} async-done(((f32[128,128]{0,1:T(8,128)}), f32[128,128]{0,1:T(8,128)}) %all-reduce.5.cloned.1.call-update) | async-done | bytes 65552 | tf_op jit(solution)/shard_map/psum | solution.py:82
  1268.1 0.9 copy.53
  1269.0 0.9 fusion.7
  1269.9 11.7 cholesky.55
  1281.6 0.6 compare_reduce_fusion
  1282.3 0.7 fusion.5
  1282.9 9.8 custom-call.9
  1292.8 1.1 convolution_multiply_fusion
  (17 shorter events, 0.2 us)
Async XLA Ops:
  6.5 1.2 copy-start
  6.5 65.3 %all-gather.6.cloned.1.call-start = ((), (), s32[]{:S(2)}) async-start(), calls=%async_computation.4 | async-start | bytes 4456448 | tf_op jit(solution)/shard_map/all_gather | solution.py:57
  8.5 156.2 %all-gather.4.cloned.1.call-start = ((), (), s32[]{:S(2)}) async-start(), calls=%async_computation.3 | async-start | bytes 8650752 | tf_op jit(solution)/shard_map/all_gather | solution.py:58
  9.3 451.6 %reduce-scatter.3.cloned.1.call-start = ((), (), s32[]{:S(2)}) async-start(), calls=%async_computation.5 | async-start | bytes 2162688 | tf_op jit(solution)/shard_map/reduce_scatter | solution.py:80
  249.9 482.6 %all-reduce.3.cloned.1.call-start = ((), (), s32[]{:S(2)}) async-start(), calls=%async_computation.6 | async-start | bytes 131072 | tf_op jit(solution)/shard_map/psum | solution.py:82
  462.8 533.7 %reduce-scatter.5.cloned.1.call-start = ((), (), s32[]{:S(2)}) async-start(), calls=%async_computation.7 | async-start | bytes 2162688 | tf_op jit(solution)/shard_map/reduce_scatter | solution.py:80
  784.8 483.3 %all-reduce.5.cloned.1.call-start = ((), (), s32[]{:S(2)}) async-start(), calls=%async_computation.8 | async-start | bytes 131072 | tf_op jit(solution)/shard_map/psum | solution.py:82
Sparse Core Ops, SparseCore 0:
  9.5 50.3 all-gather.5
  63.0 101.6 all-gather.3
  250.1 210.7 reduce-scatter.2
  465.7 266.7 all-reduce.2
  784.9 211.4 reduce-scatter.4
  1001.3 266.7 all-reduce.4
